TPU v7x, 32 devices: a whole 2x2x4 slice. The times are simulated.
32 devices in a mesh: vocab: 16 (over z, x, core), seq: 2 (over y).
Axes of the slice: x: 2, y: 2, z: 4, core: 2. Of those that a mesh axis runs over, the one named last changes fastest.
Arguments:
- hidden_states: bfloat16 [512, 3584], P('seq', 'vocab'), may hold values from -6 to 6
- norm_gain: float32 [3584], replicated, may hold values from 0.5 to 1.5
- embedding: bfloat16 [256000, 3584], P(('vocab', 'seq')), may hold values from -0.29882812 to 0.29882812
- targets: int32 [512], replicated, may hold values from 0 to 255999
Outputs:
- token_loss: float32 [512], P('seq')
- mean_loss: float32 [], replicated
All inputs are finite; a program needn't handle non-finite values.
Results may differ from a plain program's by a relative error of at most 0.0005.
Values may be sent and summed in bfloat16 or wider, within the bound.
A program may use at most 128 MiB of HBM per device.

v0:
```python
import jax
import jax.numpy as jnp
from jax import lax
from jax.sharding import PartitionSpec as P


def normalize(rows, norm_gain):
    values = rows.astype(jnp.float32)
    meansq = jnp.mean(values * values, axis=-1, keepdims=True)
    return (values * lax.rsqrt(meansq + 1e-06) * norm_gain).astype(jnp.bfloat16)


def vocab_terms_of(embedding, targets, normed_rows):
    local_rows = embedding.shape[0]
    base = (lax.axis_index("vocab") * lax.axis_size("seq") + lax.axis_index("seq")) * local_rows
    scores = jnp.einsum("vd,td->vt", embedding, normed_rows, preferred_element_type=jnp.float32)
    capped = 30.0 * jnp.tanh(scores / 30.0)
    total = jnp.sum(jnp.exp(capped), axis=0)
    ids = base + jnp.arange(local_rows, dtype=jnp.int32)
    hit = ids[:, None] == targets[None, :]
    picked = jnp.sum(jnp.where(hit, capped, 0.0), axis=0)
    return (total, picked)


def local(hidden_states, norm_gain, embedding, targets):
    own_count = hidden_states.shape[0]
    all_count = targets.shape[0]
    gathered_rows = lax.all_gather(hidden_states, "seq", axis=0, tiled=True)
    whole = lax.all_gather(gathered_rows, "vocab", axis=1, tiled=True)
    normed = normalize(whole, norm_gain)
    total, picked = vocab_terms_of(embedding, targets, normed)
    total, picked = lax.psum((total, picked), ("vocab", "seq"))
    every_loss = jnp.log(total) - picked
    mean_loss = jnp.sum(every_loss) / all_count
    token_loss = lax.dynamic_slice_in_dim(every_loss, lax.axis_index("seq") * own_count, own_count)
    return (token_loss, mean_loss)


def solution(mesh):
    placed = (P("seq", "vocab"), P(), P(("vocab", "seq"), None), P())
    return jax.shard_map(
        local, mesh=mesh, in_specs=placed, out_specs=(P("seq"), P()), check_vma=False
    )
```

profile of v0, /device:TPU:0, one launch (start us, length us, event | category | flops | bytes accessed | tf_op | source)
XLA Modules:
  0.0 157.3 jit_solution(12015956932428505481)
XLA Ops:
  7.2 0.0 all-gather.2.cloned.1.call-start
  7.2 8.7 %all_gather.6 = bf16[512,224]{0,1:T(8,128)(2,1)} all-gather(bf16[256,224]{0,1:T(8,128)(2,1)} %param.4), channel_id=1, replica_groups=mesh['vocab'=16,'seq'=2] {'seq'}, dimensions={0}, use_global_device_ids=true | all-gather | bytes 344064 | tf_op jit(solution)/shard_map/all_gather | solution.py:28
  15.9 0.0 all-gather.2.cloned.1.call-update
  15.9 48.1 %all-gather.2.cloned.1.call-done = bf16[512,3584]{0,1:T(8,128)(2,1)} async-done(((bf16[512,224]{0,1:T(8,128)(2,1)}), bf16[512,3584]{0,1:T(8,128)(2,1)}) %all-gather.2.cloned.1.call-update) | async-done | bytes 3670032 | tf_op jit(solution)/shard_map/all_gather | solution.py:29
  64.0 2.9 %fusion.2 = f32[512]{0:T(512)S(1)} fusion(bf16[512,3584]{0,1:T(8,128)(2,1)} %all-gather.2.cloned.1.call-done), kind=kLoop, calls=%fused_computation.7 | loop fusion | flops 5504512 | bytes 3672064 | tf_op jit(solution)/shard_map/reduce_sum | solution.py:9
  66.9 41.1 %fusion = (f32[512]{0:T(512)S(1)}, f32[512]{0:T(512)S(1)}) fusion(s32[512]{0:T(512)} %param.7, s32[8000]{0:T(1024)S(1)} %iota_add_fusion, bf16[8000,3584]{1,0:T(8,128)(2,1)} %param.6, bf16[512,3584]{0,1:T(8,128)(2,1)} %all-gather.2.cloned.1.call-done, f32[3584]{0:T(1024)} %param.5, f32[512]{0:T(512)S(1)} %add_rsqrt_fusion), kind=kOutput, calls=%fused_computation.2 | convolution fusion | flops 29392044032 | bytes 61068544 | tf_op jit(solution)/shard_map/vd,td->vt/dot_general | solution.py:16
  108.0 39.4 %all-reduce = (f32[512]{0:T(512)S(1)}, f32[512]{0:T(512)S(1)}) all-reduce(f32[512]{0:T(512)S(1)} %get-tuple-element.3, f32[512]{0:T(512)S(1)} %get-tuple-element.2), channel_id=1, replica_groups=mesh['vocab'=16,'seq'=2] {'vocab','seq'}, use_global_device_ids=true, to_apply=%region_4.5 | all-reduce | flops 1024 | bytes 8192 | tf_op jit(solution)/shard_map/psum | solution.py:32
  147.4 0.6 fusion.8
  148.7 0.6 dynamic_slice.3
  (2 shorter events, 0.0 us)
Async XLA Ops:
  7.2 56.8 %all-gather.2.cloned.1.call-start = ((), (), s32[]{:S(2)}) async-start(), calls=%async_computation | async-start | bytes 3899392 | tf_op jit(solution)/shard_map/all_gather | solution.py:29
Sparse Core Ops, SparseCore 0:
  16.0 47.9 all-gather.1
where the time goes:
time: 158 us; the launch traced here: 157 us
  blocking collectives  48.1 us (30%)
  waiting for transfers between devices  48.1 us (30%)
  matrix products  41.1 us (26%)
  between operations  15.8 us (10%)
  other arithmetic  3.5 us (2%)
    all_gather x1, waiting for transfers between devices, local(): whole = lax.all_gather(gathered_rows, 'vocab', axis=1, tiled=True)  48.1 us
    dot_general x1, matrix products, vocab_terms_of(): jnp.einsum('vd,td->vt', embedding, normed_rows, preferred_element_type=jn...  41.1 us
    psum x1, blocking collectives, local(): total, picked = lax.psum((total, picked), ('vocab', 'seq'))  39.4 us
    all_gather x1, blocking collectives, local(): gathered_rows = lax.all_gather(hidden_states, 'seq', axis=0, tiled=True)  8.67 us
  transfers between devices with their start and end apart: 1, of which 1 were waited for; matrix products, arithmetic and copies ran while one was open for 0% of the time, Pallas kernels for 0%

commit v1 on v0

v1 whole, which is shorter than its diff:
```python
import functools

import jax
import jax.numpy as jnp
from jax import lax
from jax.experimental import pallas as pl
from jax.experimental.pallas import tpu as pltpu
from jax.sharding import PartitionSpec as P

LANES = 128
SLOTS = 3
LOG2E = 1.4426950408889634


def tile_rows(rows, limit):
    best = rows
    for unit in (16, 8):
        sizes = [n for n in range(unit, limit + 1, unit) if rows % n == 0]
        if sizes:
            return max(sizes)
    return best


def kernel(cfg, ht_ref, gain_ref, targets_ref, emb_ref, loss_ref, mean_ref,
           raw, normed, acc, buf_a, buf_b, stat, rbuf, fin1, fin2, lossbuf, sums,
           z_send, z_recv, p_send, p_recv, c_send, c_recv, s_send, s_recv,
           f1_send, f1_recv, f2_send, f2_recv, own_sem, a_sem, b_sem):
    nv, ns, group, planes, width, own, tokens, rows, tm, features, sub = cfg
    v, s = lax.axis_index("vocab"), lax.axis_index("seq")
    p, q = v // group, v % group
    core = q % 2
    half = (group // 2) * ns
    hidx = (q // 2) * ns + s
    count = nv * ns
    me = s * nv + v
    gw = group * width
    tiles = rows // tm

    def plane_of(k):
        return (p + k) % planes

    def remote(src, dst, send, recv, vv, ss):
        return pltpu.make_async_remote_copy(
            src_ref=src, dst_ref=dst, send_sem=send, recv_sem=recv,
            device_id={"vocab": vv, "seq": ss},
            device_id_type=pl.DeviceIdType.MESH)

    first = planes - 2

    def a_copy(k, i, slot):
        col = pl.multiple_of(plane_of(k) * gw, LANES)
        row = pl.multiple_of(i * tm, 8)
        return pltpu.make_async_copy(
            emb_ref.at[pl.ds(row, tm), pl.ds(col, gw)], buf_a.at[slot], a_sem.at[slot])

    def b_copy(i, slot, part):
        col = pl.multiple_of(plane_of(first + part) * gw, LANES)
        row = pl.multiple_of(i * tm, 8)
        return pltpu.make_async_copy(
            emb_ref.at[pl.ds(row, tm), pl.ds(col, gw)],
            buf_b.at[slot, :, pl.ds(part * gw, gw)], b_sem.at[slot, part])

    total_a = first * tiles

    def a_start(n):
        for k in range(first):
            @pl.when((n >= k * tiles) & (n < (k + 1) * tiles))
            def _():
                a_copy(k, n - k * tiles, n % SLOTS).start()

    for n in range(min(SLOTS - 1, total_a)):
        a_copy(n // tiles, n % tiles, n % SLOTS).start()
    for n in range(min(SLOTS - 1, tiles)):
        for part in range(2):
            b_copy(n, n, part).start()

    h = ht_ref[...].astype(jnp.float32)
    stat[me] = jnp.sum(h * h, axis=0, keepdims=True)

    barrier = pltpu.get_barrier_semaphore()

    def greet(d, _):
        peer = (me + d) % count
        pl.semaphore_signal(barrier, inc=1,
                            device_id={"vocab": peer % nv, "seq": peer // nv},
                            device_id_type=pl.DeviceIdType.MESH)
        return 0

    lax.fori_loop(1, count, greet, 0)
    pl.semaphore_wait(barrier, count - 1)

    def tile_at(k, qq, ss):
        return raw.at[k, pl.ds(pl.multiple_of(qq * width, 16), width),
                      pl.ds(pl.multiple_of(ss * own, LANES), own)]

    def own_of(k):
        return ht_ref if k == 0 else tile_at(k, q, s)

    def z_copy(k):
        target = (p + planes - k) % planes
        return remote(ht_ref, tile_at(k, q, s), z_send.at[k], z_recv.at[k],
                      target * group + q, s)

    def p_copy(k, j):
        other = (hidx + j) % half
        return remote(own_of(k), tile_at(k, q, s), p_send.at[k, j], p_recv.at[k, j],
                      p * group + 2 * (other // ns) + core, other % ns)

    def c_copy(k, j):
        tile = (hidx + half - j) % half
        place = tile_at(k, 2 * (tile // ns) + core, tile % ns)
        return remote(place, place, c_send.at[k, j], c_recv.at[k, j],
                      p * group + (q + 1 - 2 * core), s)

    def c_own(k):
        return remote(own_of(k), tile_at(k, q, s), c_send.at[k, 0], c_recv.at[k, 0],
                      p * group + (q + 1 - 2 * core), s)

    def s_copy(d):
        peer = (me + d) % count
        return remote(stat.at[me], stat.at[me], s_send.at[d], s_recv.at[d],
                      peer % nv, peer // nv)

    def loop(low, high, action):
        def body(i, _):
            action(i)
            return 0
        lax.fori_loop(low, high, body, 0)

    def spread(k):
        loop(1, half, lambda j: p_copy(k, j).start())
        c_own(k).start()

    def relay(k):
        def one(j):
            p_copy(k, j).wait_recv()
            c_copy(k, j).start()
        loop(1, half, one)

    loop(1, count, lambda d: s_copy(d).start())
    spread(0)
    for k in range(1, planes):
        z_copy(k).start()
    own_copy = pltpu.make_async_copy(ht_ref, tile_at(0, q, s), own_sem)
    own_copy.start()

    loop(1, count, lambda d: s_copy(d).wait_recv())
    for t in range(ns):
        part = stat[t * nv:(t + 1) * nv]
        meansq = jnp.sum(part, axis=0) / features
        rbuf[:, t * own:(t + 1) * own] = lax.rsqrt(meansq + 1e-06)

    relay(0)

    def normalize(k):
        loop(0, half, lambda j: c_copy(k, j).wait_recv())
        for i in range(gw // LANES):
            row = plane_of(k) * (gw // LANES) + i
            gain = jnp.broadcast_to(gain_ref[pl.ds(row, 1), :], (LANES, LANES)).T
            for c in range(tokens // LANES):
                cols = slice(c * LANES, (c + 1) * LANES)
                values = raw[k, i * LANES:(i + 1) * LANES, cols].astype(jnp.float32)
                out = values * rbuf[:, cols] * gain
                normed[k * gw + i * LANES:k * gw + (i + 1) * LANES, cols] = (
                    out.astype(jnp.bfloat16))

    own_copy.wait()
    normalize(0)

    def step_a(k, i):
        n = k * tiles + i
        a_copy(k, i, n % SLOTS).wait()

        @pl.when(n + SLOTS - 1 < total_a)
        def _():
            a_start(n + SLOTS - 1)

        place = pl.ds(pl.multiple_of(i * tm, 8), tm)
        product = jnp.dot(buf_a[n % SLOTS], normed[k * gw:(k + 1) * gw, :],
                          preferred_element_type=jnp.float32)
        if k == 0:
            acc[place, :] = product
        else:
            acc[place, :] += product

    base = (v * ns + s) * rows

    def step_b(i):
        slot = i % SLOTS
        for part in range(2):
            b_copy(i, slot, part).wait()

        @pl.when(i + SLOTS - 1 < tiles)
        def _():
            for part in range(2):
                b_copy(i + SLOTS - 1, (i + SLOTS - 1) % SLOTS, part).start()

        total = sums[0:8, :]
        picked = sums[8:16, :]
        for m in range(tm // sub):
            place = pl.ds(pl.multiple_of(i * tm + m * sub, 8), sub)
            scores = jnp.dot(buf_b[slot, m * sub:(m + 1) * sub, :],
                             normed[first * gw:planes * gw, :],
                             preferred_element_type=jnp.float32)
            if first > 0:
                scores = scores + acc[place, :]
            bent = jnp.tanh(scores * (1.0 / 30.0))
            grown = jnp.exp2(bent * (30.0 * LOG2E))
            want = targets_ref[...] - (base + i * tm + m * sub)
            hit = lax.broadcasted_iota(jnp.int32, (sub, tokens), 0) == want
            mine = jnp.where(hit, bent, 0.0)
            total = total + jnp.sum(grown.reshape(sub // 8, 8, tokens), axis=0)
            picked = picked + jnp.sum(mine.reshape(sub // 8, 8, tokens), axis=0)
        sums[0:8, :] = total
        sums[8:16, :] = picked

    middle = tiles // 2

    def ready(k):
        if k < planes:
            z_copy(k).wait_recv()
            spread(k)

    sums[...] = jnp.zeros_like(sums)
    for k in range(first):
        nexts = [k + 1] if k + 1 < first else [k + 1, k + 2]
        for e in nexts:
            ready(e)
        loop(0, middle, functools.partial(step_a, k))
        for e in nexts:
            relay(e)
        loop(middle, tiles, functools.partial(step_a, k))
        for e in nexts:
            normalize(e)
    loop(0, tiles, step_b)

    fleet = group * ns
    pos = q * ns + s

    def f1_copy(d):
        other = (pos + d) % fleet
        return remote(fin1.at[pos], fin1.at[pos], f1_send.at[d], f1_recv.at[d],
                      p * group + other // ns, other % ns)

    def f2_copy(d):
        other = (p + d) % planes
        return remote(fin2.at[p], fin2.at[p], f2_send.at[d], f2_recv.at[d],
                      other * group + q, s)

    fin1[pos, 0:1, :] = jnp.sum(sums[0:8, :], axis=0, keepdims=True)
    fin1[pos, 1:2, :] = jnp.sum(sums[8:16, :], axis=0, keepdims=True)
    loop(1, fleet, lambda d: f1_copy(d).start())
    loop(1, fleet, lambda d: f1_copy(d).wait_recv())
    fin2[p] = jnp.sum(fin1[...], axis=0)
    loop(1, planes, lambda d: f2_copy(d).start())
    loop(1, planes, lambda d: f2_copy(d).wait_recv())
    both = jnp.sum(fin2[...], axis=0)
    losses = jnp.log(both[0:1, :]) - 30.0 * both[1:2, :]
    lossbuf[...] = losses
    mean_ref[...] = jnp.sum(losses, axis=1, keepdims=True) / tokens
    loss_ref[...] = lossbuf[:, pl.ds(pl.multiple_of(s * own, LANES), own)]

    loop(1, count, lambda d: s_copy(d).wait_send())
    for k in range(planes):
        if k > 0:
            z_copy(k).wait_send()
        loop(1, half, lambda j: p_copy(k, j).wait_send())
        loop(0, half, lambda j: c_copy(k, j).wait_send())
    loop(1, fleet, lambda d: f1_copy(d).wait_send())
    loop(1, planes, lambda d: f2_copy(d).wait_send())


def local(nv, ns, hidden_states, norm_gain, embedding, targets):
    own, width = hidden_states.shape
    rows, features = embedding.shape
    tokens = targets.shape[0]
    group = 2
    while (group * width) % LANES:
        group *= 2
    planes = nv // group
    gw = group * width
    tm = tile_rows(rows, 800)
    sub = tile_rows(tm, 400)
    half = (group // 2) * ns
    fleet = group * ns
    count = nv * ns
    cfg = (nv, ns, group, planes, width, own, tokens, rows, tm, features, sub)
    dma = pltpu.SemaphoreType.DMA
    vmem = pl.BlockSpec(memory_space=pltpu.VMEM)
    loss, mean = pl.pallas_call(
        functools.partial(kernel, cfg),
        out_shape=(jax.ShapeDtypeStruct((1, own), jnp.float32),
                   jax.ShapeDtypeStruct((1, 1), jnp.float32)),
        in_specs=[vmem, vmem, vmem, pl.BlockSpec(memory_space=pl.ANY)],
        out_specs=(vmem, vmem),
        scratch_shapes=[
            pltpu.VMEM((planes, gw, tokens), jnp.bfloat16),
            pltpu.VMEM((features, tokens), jnp.bfloat16),
            pltpu.VMEM((rows, tokens), jnp.float32),
            pltpu.VMEM((SLOTS, tm, gw), jnp.bfloat16),
            pltpu.VMEM((SLOTS, tm, 2 * gw), jnp.bfloat16),
            pltpu.VMEM((count, 1, own), jnp.float32),
            pltpu.VMEM((1, tokens), jnp.float32),
            pltpu.VMEM((fleet, 2, tokens), jnp.float32),
            pltpu.VMEM((planes, 2, tokens), jnp.float32),
            pltpu.VMEM((1, tokens), jnp.float32),
            pltpu.VMEM((16, tokens), jnp.float32),
            dma((planes,)), dma((planes,)),
            dma((planes, half)), dma((planes, half)),
            dma((planes, half)), dma((planes, half)),
            dma((count,)), dma((count,)),
            dma((fleet,)), dma((fleet,)),
            dma((planes,)), dma((planes,)),
            dma, dma((SLOTS,)), dma((SLOTS, 2)),
        ],
        compiler_params=pltpu.CompilerParams(
            collective_id=0, has_side_effects=True, vmem_limit_bytes=60 * 2**20),
    )(hidden_states.T, norm_gain.reshape(-1, LANES), targets.reshape(1, -1), embedding)
    return loss.reshape(own), mean.reshape(())


def solution(mesh):
    placed = (P("seq", "vocab"), P(), P(("vocab", "seq"), None), P())
    body = functools.partial(local, mesh.shape["vocab"], mesh.shape["seq"])
    return jax.shard_map(
        body, mesh=mesh, in_specs=placed, out_specs=(P("seq"), P()), check_vma=False
    )
```

time: 158 us -> 78.3 us (0.50)
  Pallas kernels: 0 us -> 74.5 us
  blocking collectives: 48.1 us -> 0 us
  waiting for transfers between devices: 48.1 us -> 0 us
  matrix products: 41.1 us -> 0 us
  between operations: 15.8 us -> 2.4 us
  other arithmetic: 3.5 us -> 0 us
    pallas_call x0 -> x1, Pallas kernels: none -> 74.5 us  [local(): pl.pallas_call(functools.partial(kernel, cfg), out_shape=(jax.ShapeDtypeS...]
    all_gather x1 -> x0, waiting for transfers between devices: 48.1 us -> none  [local(): whole = lax.all_gather(gathered_rows, 'vocab', axis=1, tiled=True)]
    dot_general x1 -> x0, matrix products: 41.1 us -> none  [vocab_terms_of(): jnp.einsum('vd,td->vt', embedding, normed_rows, preferred_element_type=jn...]
    psum x1 -> x0, blocking collectives: 39.4 us -> none  [local(): total, picked = lax.psum((total, picked), ('vocab', 'seq'))]
    all_gather x1 -> x0, blocking collectives: 8.67 us -> none  [local(): gathered_rows = lax.all_gather(hidden_states, 'seq', axis=0, tiled=True)]
    reduce_sum x2 -> x0, other arithmetic: 3.49 us -> none  [the longest x1 2.88 us: normalize(): meansq = jnp.mean(values * values, axis=-1, keepdims=True)]
  transfers between devices with their start and end apart: 1 -> 0, of which waited for: 1 -> 0; matrix products, arithmetic and copies ran while one was open for 0% -> 0% of each run, Pallas kernels for 0% -> 0%
where the time goes in v1:
time: 78.3 us; the launch traced here: 78.1 us
  Pallas kernels  74.5 us (95%)
  between operations  2.4 us (3%)
  local copies, waits for them, and re-layouts  1.22 us (2%)
    pallas_call x1, Pallas kernels, local(): pl.pallas_call(functools.partial(kernel, cfg), out_shape=(jax.ShapeDtypeS...  74.5 us

profile of v1, /device:TPU:0, one launch (start us, length us, event | category | flops | bytes accessed | tf_op | source)
XLA Modules:
  0.0 78.1 jit_solution(1295086542002437197)
XLA Ops:
  0.6 74.5 %shard_map.59 = (f32[1,256]{1,0:T(1,128)}, f32[1,1]{1,0:T(1,128)}) custom-call(bf16[224,256]{1,0:T(8,128)(2,1)} %bitcast.5, f32[28,128]{1,0:T(8,128)} %bitcast.6, s32[1,512]{1,0:T(1,128)} %bitcast.7, bf16[8000,3584]{1,0:T(8,128)(2,1)} %emb_ref.1), custom_call_target="tpu_custom_call" | custom-call | tf_op jit(solution)/shard_map/pallas_call | solution.py:290
  75.1 1.2 %copy.8 = f32[256]{0:T(256)} copy(f32[256]{0:T(256)} %bitcast.8) | data formatting | bytes 2048

commit v2 on v1

--- a/solution.py
+++ b/solution.py
@@ -22,9 +22,9 @@
 
 
 def kernel(cfg, ht_ref, gain_ref, targets_ref, emb_ref, loss_ref, mean_ref,
-           raw, normed, acc, buf_a, buf_b, stat, rbuf, fin1, fin2, lossbuf, sums,
+           raw, normed, acc, buf_a, buf_b, gcol, stat, rbuf, fin, lossbuf, sums,
            z_send, z_recv, p_send, p_recv, c_send, c_recv, s_send, s_recv,
-           f1_send, f1_recv, f2_send, f2_recv, own_sem, a_sem, b_sem):
+           f_send, f_recv, own_sem, a_sem, b_sem):
     nv, ns, group, planes, width, own, tokens, rows, tm, features, sub = cfg
     v, s = lax.axis_index("vocab"), lax.axis_index("seq")
     p, q = v // group, v % group
@@ -74,9 +74,6 @@
         for part in range(2):
             b_copy(n, n, part).start()
 
-    h = ht_ref[...].astype(jnp.float32)
-    stat[me] = jnp.sum(h * h, axis=0, keepdims=True)
-
     barrier = pltpu.get_barrier_semaphore()
 
     def greet(d, _):
@@ -87,6 +84,14 @@
         return 0
 
     lax.fori_loop(1, count, greet, 0)
+    h = ht_ref[...].astype(jnp.float32)
+    stat[me] = jnp.sum(h * h, axis=0, keepdims=True)
+
+    for k in range(planes):
+        for i in range(gw // LANES):
+            row = plane_of(k) * (gw // LANES) + i
+            gcol[k * gw + i * LANES:k * gw + (i + 1) * LANES, :] = jnp.broadcast_to(
+                gain_ref[pl.ds(row, 1), :], (LANES, LANES)).T
     pl.semaphore_wait(barrier, count - 1)
 
     def tile_at(k, qq, ss):
@@ -155,8 +160,7 @@
     def normalize(k):
         loop(0, half, lambda j: c_copy(k, j).wait_recv())
         for i in range(gw // LANES):
-            row = plane_of(k) * (gw // LANES) + i
-            gain = jnp.broadcast_to(gain_ref[pl.ds(row, 1), :], (LANES, LANES)).T
+            gain = gcol[k * gw + i * LANES:k * gw + (i + 1) * LANES, :]
             for c in range(tokens // LANES):
                 cols = slice(c * LANES, (c + 1) * LANES)
                 values = raw[k, i * LANES:(i + 1) * LANES, cols].astype(jnp.float32)
@@ -214,47 +218,40 @@
         sums[0:8, :] = total
         sums[8:16, :] = picked
 
-    middle = tiles // 2
-
     def ready(k):
-        if k < planes:
-            z_copy(k).wait_recv()
-            spread(k)
+        z_copy(k).wait_recv()
+        spread(k)
 
     sums[...] = jnp.zeros_like(sums)
+    ready(1)
     for k in range(first):
         nexts = [k + 1] if k + 1 < first else [k + 1, k + 2]
-        for e in nexts:
-            ready(e)
-        loop(0, middle, functools.partial(step_a, k))
-        for e in nexts:
-            relay(e)
-        loop(middle, tiles, functools.partial(step_a, k))
+        events = []
+        if k == 0:
+            events += [((e - 1) * tiles // planes, ready, e) for e in range(2, planes)]
+        marks = (6,) if len(nexts) == 1 else (4, 9)
+        events += [(mark * tiles // 10, relay, e) for mark, e in zip(marks, nexts)]
+        done = 0
+        for at, action, e in sorted(events, key=lambda event: event[0]):
+            if at > done:
+                loop(done, at, functools.partial(step_a, k))
+                done = at
+            action(e)
+        loop(done, tiles, functools.partial(step_a, k))
         for e in nexts:
             normalize(e)
     loop(0, tiles, step_b)
 
-    fleet = group * ns
-    pos = q * ns + s
-
-    def f1_copy(d):
-        other = (pos + d) % fleet
-        return remote(fin1.at[pos], fin1.at[pos], f1_send.at[d], f1_recv.at[d],
-                      p * group + other // ns, other % ns)
-
-    def f2_copy(d):
-        other = (p + d) % planes
-        return remote(fin2.at[p], fin2.at[p], f2_send.at[d], f2_recv.at[d],
-                      other * group + q, s)
-
-    fin1[pos, 0:1, :] = jnp.sum(sums[0:8, :], axis=0, keepdims=True)
-    fin1[pos, 1:2, :] = jnp.sum(sums[8:16, :], axis=0, keepdims=True)
-    loop(1, fleet, lambda d: f1_copy(d).start())
-    loop(1, fleet, lambda d: f1_copy(d).wait_recv())
-    fin2[p] = jnp.sum(fin1[...], axis=0)
-    loop(1, planes, lambda d: f2_copy(d).start())
-    loop(1, planes, lambda d: f2_copy(d).wait_recv())
-    both = jnp.sum(fin2[...], axis=0)
+    def f_copy(d):
+        peer = (me + d) % count
+        return remote(fin.at[me], fin.at[me], f_send.at[d], f_recv.at[d],
+                      peer % nv, peer // nv)
+
+    fin[me, 0:1, :] = jnp.sum(sums[0:8, :], axis=0, keepdims=True)
+    fin[me, 1:2, :] = jnp.sum(sums[8:16, :], axis=0, keepdims=True)
+    loop(1, count, lambda d: f_copy(d).start())
+    loop(1, count, lambda d: f_copy(d).wait_recv())
+    both = jnp.sum(fin[...], axis=0)
     losses = jnp.log(both[0:1, :]) - 30.0 * both[1:2, :]
     lossbuf[...] = losses
     mean_ref[...] = jnp.sum(losses, axis=1, keepdims=True) / tokens
@@ -266,8 +263,7 @@
             z_copy(k).wait_send()
         loop(1, half, lambda j: p_copy(k, j).wait_send())
         loop(0, half, lambda j: c_copy(k, j).wait_send())
-    loop(1, fleet, lambda d: f1_copy(d).wait_send())
-    loop(1, planes, lambda d: f2_copy(d).wait_send())
+    loop(1, count, lambda d: f_copy(d).wait_send())
 
 
 def local(nv, ns, hidden_states, norm_gain, embedding, targets):
@@ -280,9 +276,8 @@
     planes = nv // group
     gw = group * width
     tm = tile_rows(rows, 800)
-    sub = tile_rows(tm, 400)
+    sub = tile_rows(tm, 200)
     half = (group // 2) * ns
-    fleet = group * ns
     count = nv * ns
     cfg = (nv, ns, group, planes, width, own, tokens, rows, tm, features, sub)
     dma = pltpu.SemaphoreType.DMA
@@ -299,18 +294,17 @@
             pltpu.VMEM((rows, tokens), jnp.float32),
             pltpu.VMEM((SLOTS, tm, gw), jnp.bfloat16),
             pltpu.VMEM((SLOTS, tm, 2 * gw), jnp.bfloat16),
+            pltpu.VMEM((features, LANES), jnp.float32),
             pltpu.VMEM((count, 1, own), jnp.float32),
             pltpu.VMEM((1, tokens), jnp.float32),
-            pltpu.VMEM((fleet, 2, tokens), jnp.float32),
-            pltpu.VMEM((planes, 2, tokens), jnp.float32),
+            pltpu.VMEM((count, 2, tokens), jnp.float32),
             pltpu.VMEM((1, tokens), jnp.float32),
             pltpu.VMEM((16, tokens), jnp.float32),
             dma((planes,)), dma((planes,)),
             dma((planes, half)), dma((planes, half)),
             dma((planes, half)), dma((planes, half)),
             dma((count,)), dma((count,)),
-            dma((fleet,)), dma((fleet,)),
-            dma((planes,)), dma((planes,)),
+            dma((count,)), dma((count,)),
             dma, dma((SLOTS,)), dma((SLOTS, 2)),
         ],
         compiler_params=pltpu.CompilerParams(

time: 78.3 us -> 69.5 us (0.89)
  Pallas kernels: 74.5 us -> 65.7 us
    pallas_call x1, Pallas kernels: 74.5 us -> 65.7 us  [local(): pl.pallas_call(functools.partial(kernel, cfg), out_shape=(jax.ShapeDtypeS...]
where the time goes in v2:
time: 69.5 us; the launch traced here: 69.3 us
  Pallas kernels  65.7 us (95%)
  between operations  2.4 us (3%)
  local copies, waits for them, and re-layouts  1.22 us (2%)
    pallas_call x1, Pallas kernels, local(): pl.pallas_call(functools.partial(kernel, cfg), out_shape=(jax.ShapeDtypeS...  65.7 us

profile of v2, /device:TPU:0, one launch (start us, length us, event | category | flops | bytes accessed | tf_op | source)
XLA Modules:
  0.0 69.3 jit_solution(6697762820645984578)
XLA Ops:
  0.6 65.7 %shard_map.59 = (f32[1,256]{1,0:T(1,128)}, f32[1,1]{1,0:T(1,128)}) custom-call(bf16[224,256]{1,0:T(8,128)(2,1)} %bitcast.5, f32[28,128]{1,0:T(8,128)} %bitcast.6, s32[1,512]{1,0:T(1,128)} %bitcast.7, bf16[8000,3584]{1,0:T(8,128)(2,1)} %emb_ref.1), custom_call_target="tpu_custom_call" | custom-call | tf_op jit(solution)/shard_map/pallas_call | solution.py:285
  66.3 1.2 %copy.8 = f32[256]{0:T(256)} copy(f32[256]{0:T(256)} %bitcast.8) | data formatting | bytes 2048
